TPU v7x, 32 devices: a whole 2x2x4 slice. The times are simulated.
32 devices in a mesh: fft: 16 (over z, x, core), scal: 2 (over y).
Axes of the slice: x: 2, y: 2, z: 4, core: 2. Of those that a mesh axis runs over, the one named last changes fastest.
Arguments:
- scalar_state: float32 [2, 2, 256, 256, 128], P('scal', None, 'fft'), may hold values from -12 to 12
- velocity: bfloat16 [3, 256, 256, 256], P(None, 'fft', 'scal'), may hold values from -6 to 6
- species: int32 [2], P('scal'), may hold values from 0 to 63
- kappa_table: float32 [64], replicated, may hold values from 0.1 to 1
- dealias_bound: int32 [2], P('scal'), may hold values from 64 to 85
Outputs:
- new_state: float32 [2, 2, 256, 256, 128], P('scal', None, 'fft')
- kappa: float32 [2], P('scal')
All inputs are finite; a program needn't handle non-finite values.
Results may differ from a plain program's by a relative error of at most 0.0027.
Values may be sent and summed in bfloat16 or wider, within the bound.
A program may use at most 128 MiB of HBM per device.

v0:
```python
import math
import jax
import jax.numpy as jnp
from jax import lax
from jax.sharding import PartitionSpec as P

cfl_number = 0.2


def twiddle(size_in, size_out, length):
    row_index = jnp.arange(size_in, dtype=jnp.int32)[:, None]
    col_index = jnp.arange(size_out, dtype=jnp.int32)[None, :]
    angles = (row_index * col_index % length).astype(jnp.float32) * (2.0 * math.pi / length)
    norming = 1.0 / math.sqrt(length)
    return (jnp.cos(angles) * norming, jnp.sin(angles) * norming)


def build_tables(length):
    half_len = length // 2
    full_cos, full_sin = twiddle(length, length, length)
    inv_cos, inv_sin = twiddle(half_len, length, length)
    weight = jnp.where(jnp.arange(half_len, dtype=jnp.int32) == 0, 1.0, 2.0).astype(jnp.float32)[
        :, None
    ]
    fwd_cos, fwd_sin = twiddle(length, half_len, length)
    listed = (full_cos, full_sin, inv_cos * weight, inv_sin * weight, fwd_cos, fwd_sin)
    return tuple((matrix.astype(jnp.bfloat16) for matrix in listed))


def product(formula, operand, matrix):
    return jnp.einsum(formula, operand, matrix, preferred_element_type=jnp.float32)


def complex_section(real_part, imag_part, cos_matrix, sin_matrix, formula, inverse):
    real_cos = product(formula, real_part, cos_matrix)
    real_sin = product(formula, real_part, sin_matrix)
    imag_cos = product(formula, imag_part, cos_matrix)
    imag_sin = product(formula, imag_part, sin_matrix)
    if inverse:
        return (real_cos - imag_sin, real_sin + imag_cos)
    return (real_cos + imag_sin, imag_cos - real_sin)


def times_wave(wavenumber, real_part, imag_part):
    new_real = (-wavenumber * imag_part.astype(jnp.float32)).astype(jnp.bfloat16)
    new_imag = (wavenumber * real_part.astype(jnp.float32)).astype(jnp.bfloat16)
    return (new_real, new_imag)


def body(scalar_state, velocity, species, kappa_table, dealias_bound):
    ky_local = scalar_state.shape[2]
    length = scalar_state.shape[3]
    half_len = length // 2
    total_count = kappa_table.shape[0]
    full_cos, full_sin, inv_cos, inv_sin, fwd_cos, fwd_sin = build_tables(length)
    ky_index = lax.axis_index("fft") * ky_local + jnp.arange(ky_local, dtype=jnp.int32)
    ky_wave = jnp.where(ky_index < half_len, ky_index, ky_index - length).astype(jnp.float32)[
        :, None, None
    ]
    kz_index = jnp.arange(length, dtype=jnp.int32)
    signed_full = jnp.where(kz_index < half_len, kz_index, kz_index - length).astype(jnp.float32)
    kz_wave = signed_full[None, :, None]
    ky_whole = signed_full[:, None, None]
    kx_wave = jnp.arange(half_len, dtype=jnp.int32).astype(jnp.float32)[None, None, :]
    ksquare = kx_wave * kx_wave + ky_wave * ky_wave + kz_wave * kz_wave
    weight = jnp.where(kx_wave == 0.0, 1.0, 2.0).astype(jnp.float32)
    cell_count = float(length) ** 3
    step_size = cfl_number * 2.0 * math.pi / length
    speeds = lax.all_gather(velocity, "scal", axis=2, tiled=True)

    def finish_inverse(halves):
        y_section = complex_section(
            halves[0], halves[1], full_cos, full_sin, "...yzx,yw->...zwx", True
        )
        y_real = y_section[0].astype(jnp.bfloat16)
        y_imag = y_section[1].astype(jnp.bfloat16)
        return product("...zwk,kx->...zwx", y_real, inv_cos) - product(
            "...zwk,kx->...zwx", y_imag, inv_sin
        )

    def gradient_set(real_part, imag_part):
        pair_real = jnp.stack([real_part, -kz_wave * imag_part]).astype(jnp.bfloat16)
        pair_imag = jnp.stack([imag_part, kz_wave * real_part]).astype(jnp.bfloat16)
        z_section = complex_section(
            pair_real, pair_imag, full_cos, full_sin, "...ykx,kz->...yzx", True
        )
        z_real = z_section[0].astype(jnp.bfloat16)
        z_imag = z_section[1].astype(jnp.bfloat16)
        came_real, came_imag = (
            lax.all_to_all(z_real, "fft", split_axis=2, concat_axis=1, tiled=True),
            lax.all_to_all(z_imag, "fft", split_axis=2, concat_axis=1, tiled=True),
        )
        x_real, x_imag = times_wave(kx_wave, came_real[0], came_imag[0])
        y_real, y_imag = times_wave(ky_whole, came_real[0], came_imag[0])
        all_real = jnp.stack([x_real, y_real, came_real[1]])
        all_imag = jnp.stack([x_imag, y_imag, came_imag[1]])
        return finish_inverse((all_real, all_imag))

    def advect(gradients):
        total = speeds[0].astype(jnp.float32) * gradients[0]
        total = total + speeds[1].astype(jnp.float32) * gradients[1]
        total = total + speeds[2].astype(jnp.float32) * gradients[2]
        return total.astype(jnp.bfloat16)

    def finish_forward(halves):
        return complex_section(halves[0], halves[1], full_cos, full_sin, "...wzk,zv->...wvk", False)

    def tendency(advected, bound):
        real_x = product("zyx,xk->zyk", advected, fwd_cos).astype(jnp.bfloat16)
        imag_x = (-product("zyx,xk->zyk", advected, fwd_sin)).astype(jnp.bfloat16)
        y_section = complex_section(real_x, imag_x, full_cos, full_sin, "zyk,yw->wzk", False)
        y_real = y_section[0].astype(jnp.bfloat16)
        y_imag = y_section[1].astype(jnp.bfloat16)
        spectral = finish_forward(
            (
                lax.all_to_all(y_real, "fft", split_axis=0, concat_axis=1, tiled=True),
                lax.all_to_all(y_imag, "fft", split_axis=0, concat_axis=1, tiled=True),
            )
        )
        dealias_mask = (ksquare <= bound * bound).astype(jnp.float32)
        return (-dealias_mask * spectral[0], -dealias_mask * spectral[1])

    scalar = 0
    start_real = scalar_state[scalar, 0]
    start_imag = scalar_state[scalar, 1]
    energy = start_real * start_real + start_imag * start_imag
    local_var = [jnp.sum(weight * energy) / cell_count]
    local_grad = [jnp.sum(weight * ksquare * energy) / cell_count]
    gradients = gradient_set(start_real, start_imag)
    magnitude = jnp.sqrt(
        gradients[0] * gradients[0] + gradients[1] * gradients[1] + gradients[2] * gradients[2]
    )
    local_peak = [jnp.max(magnitude)]
    advect_saved = [advect(gradients)]
    var_part = jnp.stack(local_var)
    grad_part = jnp.stack(local_grad)
    peak_part = jnp.stack(local_peak)
    variance, mean_grad = lax.psum((var_part, grad_part), "fft")
    peak_value = lax.pmax(peak_part, "fft")
    matches = species[:, None] == jnp.arange(total_count, dtype=jnp.int32)[None, :]
    base_kappa = jnp.sum(jnp.where(matches, kappa_table[None, :], 0.0), axis=1)
    kappa = base_kappa * peak_value * jnp.sqrt(variance) / (mean_grad + 1e-06)
    scalar = 0
    start_real = scalar_state[scalar, 0]
    start_imag = scalar_state[scalar, 1]
    factor = jnp.exp(-kappa[scalar] * ksquare * step_size)
    bound = dealias_bound[scalar].astype(jnp.float32)
    first_real, first_imag = tendency(advect_saved[scalar], bound)
    mid_real = factor * (start_real + step_size * first_real)
    mid_imag = factor * (start_imag + step_size * first_imag)
    second_real, second_imag = tendency(advect(gradient_set(mid_real, mid_imag)), bound)
    new_real = factor * start_real + 0.5 * step_size * (factor * first_real + second_real)
    new_imag = factor * start_imag + 0.5 * step_size * (factor * first_imag + second_imag)
    updated_list = [jnp.stack([new_real, new_imag])]
    return (jnp.stack(updated_list), kappa)


def solution(mesh):
    placed = (
        P("scal", None, "fft", None, None),
        P(None, "fft", "scal", None),
        P("scal"),
        P(),
        P("scal"),
    )
    return jax.shard_map(
        body,
        mesh=mesh,
        in_specs=placed,
        out_specs=(P("scal", None, "fft", None, None), P("scal")),
        check_vma=False,
    )
```

profile of v0, /device:TPU:9, one launch (start us, length us, event | category | flops | bytes accessed | tf_op | source)
XLA Modules:
  0.0 545.5 jit_solution(1776327295158472400)
XLA Ops:
  7.2 2.7 bitcast_convert_fusion
  11.2 1.6 fusion.53
  12.8 1.6 fusion.48
  14.5 2.7 copy.48
  17.1 6.5 %all-to-all-start.1 = ((bf16[2,16,256,128]{3,1,0,2:T(8,128)(2,1)}), bf16[2,16,256,128]{3,1,0,2:T(8,128)(2,1)}, u32[]{:S(2)}, u32[]{:S(2)}) async-start(bf16[2,16,256,128]{3,1,0,2:T(8,128)(2,1)} %copy.48), calls=%async_computation.1 | async-start | bytes 4194304 | tf_op jit(solution)/shard_map/all_to_all | solution.py:90
  23.7 1.6 fusion.54
  25.3 1.6 fusion.47
  26.9 2.7 copy.43
  29.6 40.2 %all-to-all-done.1 = bf16[2,16,256,128]{3,1,0,2:T(8,128)(2,1)} async-done(((bf16[2,16,256,128]{3,1,0,2:T(8,128)(2,1)}), bf16[2,16,256,128]{3,1,0,2:T(8,128)(2,1)}, u32[]{:S(2)}, u32[]{:S(2)}) %all-to-all-start.1) | async-done | bytes 2097184 | tf_op jit(solution)/shard_map/all_to_all | solution.py:90
  69.9 6.1 %all-to-all-start = ((bf16[2,16,256,128]{3,1,0,2:T(8,128)(2,1)}), bf16[2,16,256,128]{3,1,0,2:T(8,128)(2,1)S(1)}, u32[]{:S(2)}, u32[]{:S(2)}) async-start(bf16[2,16,256,128]{3,1,0,2:T(8,128)(2,1)} %copy.43), calls=%async_computation | async-start | bytes 4194304 | tf_op jit(solution)/shard_map/all_to_all | solution.py:91
  76.7 2.4 copy.49
  79.1 1.7 slice_convert_fusion.2
  82.3 39.8 %all-to-all-done = bf16[2,16,256,128]{3,1,0,2:T(8,128)(2,1)S(1)} async-done(((bf16[2,16,256,128]{3,1,0,2:T(8,128)(2,1)}), bf16[2,16,256,128]{3,1,0,2:T(8,128)(2,1)S(1)}, u32[]{:S(2)}, u32[]{:S(2)}) %all-to-all-start) | async-done | bytes 2097184 | tf_op jit(solution)/shard_map/all_to_all | solution.py:91
  126.5 4.6 fusion.58
  131.1 4.5 fusion.57
  136.5 11.1 %fusion.7 = f32[3,16,256,256]{3,2,1,0:T(8,128)} fusion(f32[256,3,16,128]{3,0,2,1:T(8,128)} %fusion.58, bf16[1,256,16,128]{3,1,2,0:T(8,128)(2,1)S(1)} %copy.56, bf16[1,256,16,128]{3,1,2,0:T(8,128)(2,1)S(1)} %get-tuple-element.27, bf16[1,256,16,128]{3,1,2,0:T(8,128)(2,1)S(1)} %get-tuple-element.26, f32[128]{0:T(128)S(1)} %fusion.137), kind=kOutput, calls=%fused_computation.28 | convolution fusion | flops 1624768512 | bytes 22020608 | tf_op jit(solution)/shard_map/...zwk,kx->...zwx/dot_general | solution.py:31
  147.5 11.4 %convolution_subtract_fusion.1 = f32[3,16,256,256]{3,2,1,0:T(8,128)} fusion(f32[3,16,256,256]{3,2,1,0:T(8,128)} %fusion.7, f32[256,3,16,128]{3,0,2,1:T(8,128)} %fusion.57, bf16[1,256,16,128]{3,1,2,0:T(8,128)(2,1)S(1)} %copy.56, bf16[1,256,16,128]{3,1,2,0:T(8,128)(2,1)S(1)} %get-tuple-element.27, bf16[1,256,16,128]{3,1,2,0:T(8,128)(2,1)S(1)} %get-tuple-element.26, ...), kind=kOutput, calls=%fused_computation.11 | convolution fusion | flops 1627914240 | bytes 34603520 | tf_op jit(solution)/shard_map/...zwk,kx->...zwx/dot_general | solution.py:31
  159.2 8.5 %sqrt_reduce_fusion = (f32[]{:T(128)}, bf16[16,256,256]{2,1,0:T(8,128)(2,1)S(1)}) fusion(f32[3,16,256,256]{3,2,1,0:T(8,128)} %convolution_subtract_fusion.1, bf16[3,16,256,256]{3,2,1,0:T(8,128)(2,1)} %all-gather.2.cloned.1.call-done), kind=kLoop, calls=%fused_computation.19 | loop fusion | flops 15728639 | bytes 20971524 | tf_op jit(solution)/shard_map/reduce_max | solution.py:133
  171.3 1.4 subtract_convert_fusion.5
  172.7 1.6 copy.59
  174.3 6.5 %all-to-all-start.3 = ((bf16[256,16,128]{2,1,0:T(8,128)(2,1)}), bf16[256,16,128]{2,1,0:T(8,128)(2,1)S(1)}, u32[]{:S(2)}, u32[]{:S(2)}) async-start(bf16[256,16,128]{2,1,0:T(8,128)(2,1)} %copy.59), calls=%async_computation.3 | async-start | bytes 2097152 | tf_op jit(solution)/shard_map/all_to_all | solution.py:117
  182.2 1.4 add_convert_fusion.5
  183.5 1.6 copy.57
  185.2 20.6 %all-to-all-done.3 = bf16[256,16,128]{2,1,0:T(8,128)(2,1)S(1)} async-done(((bf16[256,16,128]{2,1,0:T(8,128)(2,1)}), bf16[256,16,128]{2,1,0:T(8,128)(2,1)S(1)}, u32[]{:S(2)}, u32[]{:S(2)}) %all-to-all-start.3) | async-done | bytes 1048608 | tf_op jit(solution)/shard_map/all_to_all | solution.py:117
  205.8 4.8 all-to-all-start.2
  210.6 3.5 fusion.25
  215.5 35.4 %all-reduce = (f32[1]{0:T(128)}, f32[1]{0:T(128)}) all-reduce(f32[1]{0:T(128)} %bitcast.31, f32[1]{0:T(128)} %bitcast.32), channel_id=1, replica_groups=mesh['fft'=16,'scal'=2] {'fft'}, use_global_device_ids=true, to_apply=%region_4.5 | all-reduce | flops 2 | bytes 16 | tf_op jit(solution)/shard_map/psum | solution.py:138
  254.2 27.1 %pmax.7 = f32[1]{0:T(128)} all-reduce(f32[1]{0:T(128)} %bitcast.28), channel_id=1, replica_groups=mesh['fft'=16,'scal'=2] {'fft'}, use_global_device_ids=true, to_apply=%region_2.3 | all-reduce | flops 1 | bytes 8 | tf_op jit(solution)/shard_map/pmax | solution.py:139
  284.2 1.5 copy.58
  287.0 1.5 bitcast_multiply_fusion.2
  288.5 1.5 bitcast_multiply_fusion.3
  290.0 1.4 copy-done.1
  292.9 1.6 fusion.51
  294.5 1.6 fusion.50
  296.1 2.7 copy.66
  298.8 13.1 %all-to-all-start.5 = ((bf16[2,16,256,128]{3,1,0,2:T(8,128)(2,1)}), bf16[2,16,256,128]{3,1,0,2:T(8,128)(2,1)}, u32[]{:S(2)}, u32[]{:S(2)}) async-start(bf16[2,16,256,128]{3,1,0,2:T(8,128)(2,1)} %copy.66), calls=%async_computation.5 | async-start | bytes 4194304 | tf_op jit(solution)/shard_map/all_to_all | solution.py:90
  311.9 3.0 fusion.52
  314.9 1.6 fusion.49
  316.5 2.7 copy.61
  319.3 38.8 %all-to-all-done.5 = bf16[2,16,256,128]{3,1,0,2:T(8,128)(2,1)} async-done(((bf16[2,16,256,128]{3,1,0,2:T(8,128)(2,1)}), bf16[2,16,256,128]{3,1,0,2:T(8,128)(2,1)}, u32[]{:S(2)}, u32[]{:S(2)}) %all-to-all-start.5) | async-done | bytes 2097184 | tf_op jit(solution)/shard_map/all_to_all | solution.py:90
  358.1 6.1 %all-to-all-start.4 = ((bf16[2,16,256,128]{3,1,0,2:T(8,128)(2,1)}), bf16[2,16,256,128]{3,1,0,2:T(8,128)(2,1)}, u32[]{:S(2)}, u32[]{:S(2)}) async-start(bf16[2,16,256,128]{3,1,0,2:T(8,128)(2,1)} %copy.61), calls=%async_computation.4 | async-start | bytes 4194304 | tf_op jit(solution)/shard_map/all_to_all | solution.py:91
  364.2 2.4 copy.67
  366.6 1.7 slice_convert_fusion
  368.8 41.5 %all-to-all-done.4 = bf16[2,16,256,128]{3,1,0,2:T(8,128)(2,1)} async-done(((bf16[2,16,256,128]{3,1,0,2:T(8,128)(2,1)}), bf16[2,16,256,128]{3,1,0,2:T(8,128)(2,1)}, u32[]{:S(2)}, u32[]{:S(2)}) %all-to-all-start.4) | async-done | bytes 2097184 | tf_op jit(solution)/shard_map/all_to_all | solution.py:91
  410.4 2.4 copy.62
  414.3 4.6 fusion.56
  418.8 4.5 fusion.55
  425.3 1.8 multiply_convert_fusion.1
  427.2 11.9 %fusion.12 = f32[3,16,256,256]{3,2,1,0:T(8,128)} fusion(f32[256,3,16,128]{3,0,2,1:T(8,128)} %fusion.56, bf16[1,256,16,128]{3,1,2,0:T(8,128)(2,1)} %copy.74, bf16[1,256,16,128]{3,1,2,0:T(8,128)(2,1)} %get-tuple-element.19, bf16[1,256,16,128]{3,1,2,0:T(8,128)(2,1)S(1)} %get-tuple-element.18, f32[128]{0:T(128)S(1)} %fusion.137), kind=kOutput, calls=%fused_computation.31 | convolution fusion | flops 1624768512 | bytes 22020608 | tf_op jit(solution)/shard_map/...zwk,kx->...zwx/dot_general | solution.py:31
  439.1 12.0 %convolution_subtract_fusion = f32[3,16,256,256]{3,2,1,0:T(8,128)} fusion(f32[3,16,256,256]{3,2,1,0:T(8,128)} %fusion.12, f32[256,3,16,128]{3,0,2,1:T(8,128)} %fusion.55, bf16[1,256,16,128]{3,1,2,0:T(8,128)(2,1)} %copy.74, bf16[1,256,16,128]{3,1,2,0:T(8,128)(2,1)} %get-tuple-element.19, bf16[1,256,16,128]{3,1,2,0:T(8,128)(2,1)S(1)} %get-tuple-element.18, ...), kind=kOutput, calls=%fused_computation.10 | convolution fusion | flops 1627914240 | bytes 34603520 | tf_op jit(solution)/shard_map/...zwk,kx->...zwx/dot_general | solution.py:31
  451.1 7.2 %fusion.42 = bf16[16,256,256]{2,1,0:T(8,128)(2,1)S(1)} fusion(f32[3,16,256,256]{3,2,1,0:T(8,128)} %convolution_subtract_fusion, bf16[3,16,256,256]{3,2,1,0:T(8,128)(2,1)} %all-gather.2.cloned.1.call-done), kind=kLoop, calls=%fused_computation.59 | loop fusion | flops 9437184 | bytes 20971520 | tf_op jit(solution)/shard_map/add | solution.py:102
  462.1 1.4 subtract_convert_fusion.4
  463.5 1.6 copy.77
  465.1 6.4 %all-to-all-start.7 = ((bf16[256,16,128]{2,1,0:T(8,128)(2,1)}), bf16[256,16,128]{2,1,0:T(8,128)(2,1)}, u32[]{:S(2)}, u32[]{:S(2)}) async-start(bf16[256,16,128]{2,1,0:T(8,128)(2,1)} %copy.77), calls=%async_computation.7 | async-start | bytes 2097152 | tf_op jit(solution)/shard_map/all_to_all | solution.py:117
  474.2 1.7 copy.75
  475.9 20.5 %all-to-all-done.7 = bf16[256,16,128]{2,1,0:T(8,128)(2,1)} async-done(((bf16[256,16,128]{2,1,0:T(8,128)(2,1)}), bf16[256,16,128]{2,1,0:T(8,128)(2,1)}, u32[]{:S(2)}, u32[]{:S(2)}) %all-to-all-start.7) | async-done | bytes 1048608 | tf_op jit(solution)/shard_map/all_to_all | solution.py:117
  496.4 4.8 all-to-all-start.6
  501.1 1.5 copy.78
  502.6 2.7 fusion.81
  505.3 20.8 %all-to-all-done.6 = bf16[256,16,128]{2,1,0:T(8,128)(2,1)} async-done(((bf16[256,16,128]{2,1,0:T(8,128)(2,1)}), bf16[256,16,128]{2,1,0:T(8,128)(2,1)}, u32[]{:S(2)}, u32[]{:S(2)}) %all-to-all-start.6) | async-done | bytes 1048608 | tf_op jit(solution)/shard_map/all_to_all | solution.py:116
  526.2 1.6 copy.76
  529.2 3.8 fusion.39
  532.9 2.1 fusion.35
  535.0 2.3 maximum_bitcast_fusion
  (80 shorter events, 30.7 us)
Async XLA Ops:
  7.2 3.5 copy-start
  11.2 1.6 copy-start.9
  17.1 52.7 %all-to-all-start.1 = ((bf16[2,16,256,128]{3,1,0,2:T(8,128)(2,1)}), bf16[2,16,256,128]{3,1,0,2:T(8,128)(2,1)}, u32[]{:S(2)}, u32[]{:S(2)}) async-start(bf16[2,16,256,128]{3,1,0,2:T(8,128)(2,1)} %copy.48), calls=%async_computation.1 | async-start | bytes 4194304 | tf_op jit(solution)/shard_map/all_to_all | solution.py:90
  23.7 1.6 copy-start.10
  69.9 52.3 %all-to-all-start = ((bf16[2,16,256,128]{3,1,0,2:T(8,128)(2,1)}), bf16[2,16,256,128]{3,1,0,2:T(8,128)(2,1)S(1)}, u32[]{:S(2)}, u32[]{:S(2)}) async-start(bf16[2,16,256,128]{3,1,0,2:T(8,128)(2,1)} %copy.43), calls=%async_computation | async-start | bytes 4194304 | tf_op jit(solution)/shard_map/all_to_all | solution.py:91
  76.0 83.2 %all-gather.2.cloned.1.call-start = ((), (), s32[]{:S(2)}) async-start(), calls=%async_computation.8 | async-start | bytes 9437184 | tf_op jit(solution)/shard_map/all_gather | solution.py:69
  123.5 1.6 copy-start.12
  125.3 1.2 copy-start.15
  174.3 31.4 %all-to-all-start.3 = ((bf16[256,16,128]{2,1,0:T(8,128)(2,1)}), bf16[256,16,128]{2,1,0:T(8,128)(2,1)S(1)}, u32[]{:S(2)}, u32[]{:S(2)}) async-start(bf16[256,16,128]{2,1,0:T(8,128)(2,1)} %copy.59), calls=%async_computation.3 | async-start | bytes 2097152 | tf_op jit(solution)/shard_map/all_to_all | solution.py:117
  205.8 78.4 %all-to-all-start.2 = ((bf16[256,16,128]{2,1,0:T(8,128)(2,1)}), bf16[256,16,128]{2,1,0:T(8,128)(2,1)}, u32[]{:S(2)}, u32[]{:S(2)}) async-start(bf16[256,16,128]{2,1,0:T(8,128)(2,1)} %copy.57), calls=%async_computation.2 | async-start | bytes 2097152 | tf_op jit(solution)/shard_map/all_to_all | solution.py:116
  210.6 43.0 %copy-start.16 = (f32[64]{0:T(128)S(1)}, f32[64]{0:T(128)}, u32[]{:S(2)}) copy-start(f32[64]{0:T(128)} %param.8) | copy-start | bytes 772
  288.5 1.5 copy-start.3
  288.5 2.9 copy-start.1
  292.8 1.6 copy-start.4
  292.8 1.6 copy-start.5
  292.9 1.7 copy-start.7
  298.8 59.3 %all-to-all-start.5 = ((bf16[2,16,256,128]{3,1,0,2:T(8,128)(2,1)}), bf16[2,16,256,128]{3,1,0,2:T(8,128)(2,1)}, u32[]{:S(2)}, u32[]{:S(2)}) async-start(bf16[2,16,256,128]{3,1,0,2:T(8,128)(2,1)} %copy.66), calls=%async_computation.5 | async-start | bytes 4194304 | tf_op jit(solution)/shard_map/all_to_all | solution.py:90
  311.9 3.0 copy-start.6
  311.9 3.0 copy-start.8
  358.1 52.3 %all-to-all-start.4 = ((bf16[2,16,256,128]{3,1,0,2:T(8,128)(2,1)}), bf16[2,16,256,128]{3,1,0,2:T(8,128)(2,1)}, u32[]{:S(2)}, u32[]{:S(2)}) async-start(bf16[2,16,256,128]{3,1,0,2:T(8,128)(2,1)} %copy.61), calls=%async_computation.4 | async-start | bytes 4194304 | tf_op jit(solution)/shard_map/all_to_all | solution.py:91
  423.4 1.8 copy-start.11
  459.6 1.2 copy-start.13
  465.1 31.3 %all-to-all-start.7 = ((bf16[256,16,128]{2,1,0:T(8,128)(2,1)}), bf16[256,16,128]{2,1,0:T(8,128)(2,1)}, u32[]{:S(2)}, u32[]{:S(2)}) async-start(bf16[256,16,128]{2,1,0:T(8,128)(2,1)} %copy.77), calls=%async_computation.7 | async-start | bytes 2097152 | tf_op jit(solution)/shard_map/all_to_all | solution.py:117
  471.5 1.3 copy-start.14
  496.4 29.8 %all-to-all-start.6 = ((bf16[256,16,128]{2,1,0:T(8,128)(2,1)}), bf16[256,16,128]{2,1,0:T(8,128)(2,1)}, u32[]{:S(2)}, u32[]{:S(2)}) async-start(bf16[256,16,128]{2,1,0:T(8,128)(2,1)} %copy.75), calls=%async_computation.6 | async-start | bytes 2097152 | tf_op jit(solution)/shard_map/all_to_all | solution.py:116
  526.2 3.0 copy-start.2
Sparse Core Ops, SparseCore 0:
  78.3 80.8 all-gather.1
where the time goes:
time: 554 us; the launch traced here: 546 us
  waiting for transfers between devices  223 us (40%)
  matrix products  110 us (20%)
  blocking collectives  62.5 us (11%)
  starting transfers between devices  54.8 us (10%)
  local copies, waits for them, and re-layouts  41.8 us (8%)
  other arithmetic  32.5 us (6%)
  between operations  21.2 us (4%)
    dot_general x36, matrix products, product(): jnp.einsum(formula, operand, matrix, preferred_element_type=jnp.float32)  110 us
    all_to_all x2, waiting for transfers between devices, gradient_set(): lax.all_to_all(z_imag, 'fft', split_axis=2, concat_axis=1, tiled=True)  81.3 us
    all_to_all x2, waiting for transfers between devices, gradient_set(): lax.all_to_all(z_real, 'fft', split_axis=2, concat_axis=1, tiled=True)  79.1 us
    all_to_all x2, waiting for transfers between devices, tendency(): lax.all_to_all(y_imag, 'fft', split_axis=0, concat_axis=1, tiled=True)  41.1 us
    psum x1, blocking collectives, body(): variance, mean_grad = lax.psum((var_part, grad_part), 'fft')  35.4 us
    pmax x1, blocking collectives, body(): peak_value = lax.pmax(peak_part, 'fft')  27.1 us
    all_to_all x2, waiting for transfers between devices, tendency(): lax.all_to_all(y_real, 'fft', split_axis=0, concat_axis=1, tiled=True)  20.8 us
    all_to_all x2, starting transfers between devices, gradient_set(): lax.all_to_all(z_real, 'fft', split_axis=2, concat_axis=1, tiled=True)  19.6 us
  transfers between devices with their start and end apart: 9, of which 8 were waited for; matrix products, arithmetic and copies ran while one was open for 14% of the time, Pallas kernels for 0%

commit v1 on v0

--- a/solution.py
+++ b/solution.py
@@ -5,6 +5,29 @@
 from jax.sharding import PartitionSpec as P
 
 cfl_number = 0.2
+
+
+def in_blocks(value, dim, devices):
+    before, after = (value.shape[:dim], value.shape[dim + 1 :])
+    return jnp.moveaxis(value.reshape(*before, devices, -1, *after), dim, 0)
+
+
+def joined_along(tiles, dim):
+    tiles = jnp.moveaxis(tiles, 0, dim)
+    dims = tiles.shape
+    return tiles.reshape(*dims[:dim], dims[dim] * dims[dim + 1], *dims[dim + 2 :])
+
+
+def exchange_directly(shard, axis, split_dim, concat_dim):
+    size, index = (lax.axis_size(axis), lax.axis_index(axis))
+    blocks = in_blocks(shard, split_dim, size)
+    filled = blocks
+    for step in range(1, size):
+        target, source = ((index + step) % size, (index - step) % size)
+        sent = lax.dynamic_index_in_dim(blocks, target, 0)
+        other = lax.ppermute(sent, axis, [(i, (i + step) % size) for i in range(size)])
+        filled = lax.dynamic_update_slice_in_dim(filled, other, source, axis=0)
+    return joined_along(filled, concat_dim)
 
 
 def twiddle(size_in, size_out, length):
@@ -114,7 +137,7 @@
         spectral = finish_forward(
             (
                 lax.all_to_all(y_real, "fft", split_axis=0, concat_axis=1, tiled=True),
-                lax.all_to_all(y_imag, "fft", split_axis=0, concat_axis=1, tiled=True),
+                exchange_directly(y_imag, "fft", 0, 1),
             )
         )
         dealias_mask = (ksquare <= bound * bound).astype(jnp.float32)

time: 554 us -> 564 us (1.018)
  starting transfers between devices: 54.8 us -> 125 us
  waiting for transfers between devices: 223 us -> 167 us
    ppermute x0 -> x30, starting transfers between devices: none -> 86.4 us  [exchange_directly(): lax.ppermute(sent, axis, [(i, (i + step) % size) for i in range(size)])]
    all_to_all x2 -> x0, waiting for transfers between devices: 41.1 us -> none  [tendency(): lax.all_to_all(y_imag, 'fft', split_axis=0, concat_axis=1, tiled=True)]
    all_to_all x2, waiting for transfers between devices: 20.8 us -> 0.01 us  [tendency(): lax.all_to_all(y_real, 'fft', split_axis=0, concat_axis=1, tiled=True)]
    all_to_all x2 -> x0, starting transfers between devices: 12.9 us -> none  [tendency(): lax.all_to_all(y_imag, 'fft', split_axis=0, concat_axis=1, tiled=True)]
    all_to_all x2, starting transfers between devices: 19.6 us -> 12.5 us  [gradient_set(): lax.all_to_all(z_real, 'fft', split_axis=2, concat_axis=1, tiled=True)]
    ppermute x0 -> x30, waiting for transfers between devices: none -> 6.09 us  [exchange_directly(): lax.ppermute(sent, axis, [(i, (i + step) % size) for i in range(size)])]
  transfers between devices with their start and end apart: 9 -> 37, of which waited for: 8 -> 10; matrix products, arithmetic and copies ran while one was open for 14% -> 13% of each run, Pallas kernels for 0% -> 0%
where the time goes in v1:
time: 564 us; the launch traced here: 554 us
  waiting for transfers between devices  167 us (30%)
  starting transfers between devices  125 us (22%)
  matrix products  113 us (20%)
  blocking collectives  57.6 us (10%)
  local copies, waits for them, and re-layouts  39.7 us (7%)
  other arithmetic  30.7 us (5%)
  between operations  21.7 us (4%)
    dot_general x36, matrix products, product(): jnp.einsum(formula, operand, matrix, preferred_element_type=jnp.float32)  113 us
    ppermute x30, starting transfers between devices, exchange_directly(): lax.ppermute(sent, axis, [(i, (i + step) % size) for i in range(size)])  86.4 us
    all_to_all x2, waiting for transfers between devices, gradient_set(): lax.all_to_all(z_imag, 'fft', split_axis=2, concat_axis=1, tiled=True)  81.1 us
    all_to_all x2, waiting for transfers between devices, gradient_set(): lax.all_to_all(z_real, 'fft', split_axis=2, concat_axis=1, tiled=True)  79 us
    psum x1, blocking collectives, body(): variance, mean_grad = lax.psum((var_part, grad_part), 'fft')  32.7 us
    pmax x1, blocking collectives, body(): peak_value = lax.pmax(peak_part, 'fft')  24.8 us
    all_to_all x2, starting transfers between devices, tendency(): lax.all_to_all(y_real, 'fft', split_axis=0, concat_axis=1, tiled=True)  12.9 us
    all_to_all x2, starting transfers between devices, gradient_set(): lax.all_to_all(z_real, 'fft', split_axis=2, concat_axis=1, tiled=True)  12.5 us
  transfers between devices with their start and end apart: 37, of which 10 were waited for; matrix products, arithmetic and copies ran while one was open for 13% of the time, Pallas kernels for 0%

profile of v1, /device:TPU:9, one launch (start us, length us, event | category | flops | bytes accessed | tf_op | source)
XLA Modules:
  0.0 554.0 jit_solution(6600580647465836914)
XLA Ops:
  7.2 2.7 bitcast_convert_fusion
  14.5 2.7 copy.46
  17.1 6.5 %all-to-all-start.1 = ((bf16[2,16,256,128]{3,1,0,2:T(8,128)(2,1)}), bf16[2,16,256,128]{3,1,0,2:T(8,128)(2,1)}, u32[]{:S(2)}, u32[]{:S(2)}) async-start(bf16[2,16,256,128]{3,1,0,2:T(8,128)(2,1)} %copy.46), calls=%async_computation.1 | async-start | bytes 4194304 | tf_op jit(solution)/shard_map/all_to_all | solution.py:113
  26.9 2.7 copy.41
  29.7 40.2 %all-to-all-done.1 = bf16[2,16,256,128]{3,1,0,2:T(8,128)(2,1)} async-done(((bf16[2,16,256,128]{3,1,0,2:T(8,128)(2,1)}), bf16[2,16,256,128]{3,1,0,2:T(8,128)(2,1)}, u32[]{:S(2)}, u32[]{:S(2)}) %all-to-all-start.1) | async-done | bytes 2097184 | tf_op jit(solution)/shard_map/all_to_all | solution.py:113
  69.9 6.1 %all-to-all-start = ((bf16[2,16,256,128]{3,1,0,2:T(8,128)(2,1)}), bf16[2,16,256,128]{3,1,0,2:T(8,128)(2,1)S(1)}, u32[]{:S(2)}, u32[]{:S(2)}) async-start(bf16[2,16,256,128]{3,1,0,2:T(8,128)(2,1)} %copy.41), calls=%async_computation | async-start | bytes 4194304 | tf_op jit(solution)/shard_map/all_to_all | solution.py:114
  76.9 2.4 copy.47
  79.3 1.7 slice_convert_fusion.2
  82.5 39.6 %all-to-all-done = bf16[2,16,256,128]{3,1,0,2:T(8,128)(2,1)S(1)} async-done(((bf16[2,16,256,128]{3,1,0,2:T(8,128)(2,1)}), bf16[2,16,256,128]{3,1,0,2:T(8,128)(2,1)S(1)}, u32[]{:S(2)}, u32[]{:S(2)}) %all-to-all-start) | async-done | bytes 2097184 | tf_op jit(solution)/shard_map/all_to_all | solution.py:114
  126.5 4.6 fusion.58
  131.1 4.6 fusion.57
  136.5 11.1 %fusion.7 = f32[3,16,256,256]{3,2,1,0:T(8,128)} fusion(f32[256,3,16,128]{3,0,2,1:T(8,128)} %fusion.58, bf16[1,256,16,128]{3,1,2,0:T(8,128)(2,1)S(1)} %copy.54, bf16[1,256,16,128]{3,1,2,0:T(8,128)(2,1)S(1)} %get-tuple-element.27, bf16[1,256,16,128]{3,1,2,0:T(8,128)(2,1)S(1)} %get-tuple-element.26, f32[128]{0:T(128)S(1)} %fusion.177), kind=kOutput, calls=%fused_computation.28 | convolution fusion | flops 1624768512 | bytes 22020608 | tf_op jit(solution)/shard_map/...zwk,kx->...zwx/dot_general | solution.py:54
  147.6 11.4 %convolution_subtract_fusion.1 = f32[3,16,256,256]{3,2,1,0:T(8,128)} fusion(f32[3,16,256,256]{3,2,1,0:T(8,128)} %fusion.7, f32[256,3,16,128]{3,0,2,1:T(8,128)} %fusion.57, bf16[1,256,16,128]{3,1,2,0:T(8,128)(2,1)S(1)} %copy.54, bf16[1,256,16,128]{3,1,2,0:T(8,128)(2,1)S(1)} %get-tuple-element.27, bf16[1,256,16,128]{3,1,2,0:T(8,128)(2,1)S(1)} %get-tuple-element.26, ...), kind=kOutput, calls=%fused_computation.11 | convolution fusion | flops 1627914240 | bytes 34603520 | tf_op jit(solution)/shard_map/...zwk,kx->...zwx/dot_general | solution.py:54
  159.2 8.5 %sqrt_reduce_fusion = (f32[]{:T(128)}, bf16[16,256,256]{2,1,0:T(8,128)(2,1)S(1)}) fusion(f32[3,16,256,256]{3,2,1,0:T(8,128)} %convolution_subtract_fusion.1, bf16[3,16,256,256]{3,2,1,0:T(8,128)(2,1)} %all-gather.2.cloned.1.call-done), kind=kLoop, calls=%fused_computation.19 | loop fusion | flops 15728639 | bytes 20971524 | tf_op jit(solution)/shard_map/reduce_max | solution.py:156
  171.3 2.7 fusion.91
  175.4 1.7 copy.55
  177.0 6.5 %all-to-all-start.2 = ((bf16[256,16,128]{2,1,0:T(8,128)(2,1)}), bf16[256,16,128]{2,1,0:T(8,128)(2,1)}, u32[]{:S(2)}, u32[]{:S(2)}) async-start(bf16[256,16,128]{2,1,0:T(8,128)(2,1)} %copy.55), calls=%async_computation.2 | async-start | bytes 2097152 | tf_op jit(solution)/shard_map/all_to_all | solution.py:139
  183.5 3.1 subtract_convert_fusion.5
  191.2 32.7 %all-reduce = (f32[1]{0:T(128)}, f32[1]{0:T(128)}) all-reduce(f32[1]{0:T(128)} %bitcast.31, f32[1]{0:T(128)} %bitcast.32), channel_id=1, replica_groups=mesh['fft'=16,'scal'=2] {'fft'}, use_global_device_ids=true, to_apply=%region_4.5 | all-reduce | flops 2 | bytes 16 | tf_op jit(solution)/shard_map/psum | solution.py:161
  226.9 2.9 collective-permute-start.1
  230.5 24.8 %pmax.7 = f32[1]{0:T(128)} all-reduce(f32[1]{0:T(128)} %bitcast.28), channel_id=1, replica_groups=mesh['fft'=16,'scal'=2] {'fft'}, use_global_device_ids=true, to_apply=%region_2.3 | all-reduce | flops 1 | bytes 8 | tf_op jit(solution)/shard_map/pmax | solution.py:162
  256.8 2.0 collective-permute-start.2
  258.8 3.2 collective-permute-start.3
  261.9 6.9 %collective-permute-start.4 = (bf16[1,16,16,128]{3,1,0,2:T(8,128)(2,1)S(1)}, bf16[1,16,16,128]{3,1,0,2:T(8,128)(2,1)S(1)}, u32[]{:S(2)}, u32[]{:S(2)}) collective-permute-start(bf16[1,16,16,128]{3,1,0,2:T(8,128)(2,1)S(1)} %get-tuple-element.59), channel_id=1, source_target_pairs={{0,10},{2,12},{4,14},{6,16},{8,18},{10,20},{12,22},{14,24},{16,26}... | collective-permute-start | bytes 196616 | tf_op jit(solution)/shard_map/ppermute | solution.py:28
  268.8 2.9 collective-permute-start.5
  272.0 2.6 collective-permute-start.7
  274.6 2.2 collective-permute-start.8
  276.8 2.0 collective-permute-start.9
  280.2 3.3 collective-permute-start.11
  283.5 6.8 %collective-permute-start.12 = (bf16[1,16,16,128]{3,1,0,2:T(8,128)(2,1)S(1)}, bf16[1,16,16,128]{3,1,0,2:T(8,128)(2,1)S(1)}, u32[]{:S(2)}, u32[]{:S(2)}) collective-permute-start(bf16[1,16,16,128]{3,1,0,2:T(8,128)(2,1)S(1)} %get-tuple-element.51), channel_id=1, source_target_pairs={{0,26},{2,28},{4,30},{6,0},{8,2},{10,4},{12,6},{14,8},{16,10},{18,... | collective-permute-start | bytes 196616 | tf_op jit(solution)/shard_map/ppermute | solution.py:28
  290.5 1.9 collective-permute-start.14
  308.7 2.9 copy.63
  311.6 5.9 %all-to-all-start.4 = ((bf16[2,16,256,128]{3,1,0,2:T(8,128)(2,1)}), bf16[2,16,256,128]{3,1,0,2:T(8,128)(2,1)}, u32[]{:S(2)}, u32[]{:S(2)}) async-start(bf16[2,16,256,128]{3,1,0,2:T(8,128)(2,1)} %copy.63), calls=%async_computation.4 | async-start | bytes 4194304 | tf_op jit(solution)/shard_map/all_to_all | solution.py:113
  317.5 3.0 fusion.52
  322.2 2.7 copy.58
  324.9 38.8 %all-to-all-done.4 = bf16[2,16,256,128]{3,1,0,2:T(8,128)(2,1)} async-done(((bf16[2,16,256,128]{3,1,0,2:T(8,128)(2,1)}), bf16[2,16,256,128]{3,1,0,2:T(8,128)(2,1)}, u32[]{:S(2)}, u32[]{:S(2)}) %all-to-all-start.4) | async-done | bytes 2097184 | tf_op jit(solution)/shard_map/all_to_all | solution.py:113
  363.7 6.1 %all-to-all-start.3 = ((bf16[2,16,256,128]{3,1,0,2:T(8,128)(2,1)}), bf16[2,16,256,128]{3,1,0,2:T(8,128)(2,1)}, u32[]{:S(2)}, u32[]{:S(2)}) async-start(bf16[2,16,256,128]{3,1,0,2:T(8,128)(2,1)} %copy.58), calls=%async_computation.3 | async-start | bytes 4194304 | tf_op jit(solution)/shard_map/all_to_all | solution.py:114
  369.8 2.4 copy.64
  372.2 1.7 slice_convert_fusion
  374.5 41.5 %all-to-all-done.3 = bf16[2,16,256,128]{3,1,0,2:T(8,128)(2,1)} async-done(((bf16[2,16,256,128]{3,1,0,2:T(8,128)(2,1)}), bf16[2,16,256,128]{3,1,0,2:T(8,128)(2,1)}, u32[]{:S(2)}, u32[]{:S(2)}) %all-to-all-start.3) | async-done | bytes 2097184 | tf_op jit(solution)/shard_map/all_to_all | solution.py:114
  416.0 2.4 copy.59
  419.9 4.6 fusion.56
  424.5 4.6 fusion.55
  431.0 1.8 multiply_convert_fusion.1
  432.8 12.0 %fusion.12 = f32[3,16,256,256]{3,2,1,0:T(8,128)} fusion(f32[256,3,16,128]{3,0,2,1:T(8,128)} %fusion.56, bf16[1,256,16,128]{3,1,2,0:T(8,128)(2,1)} %copy.71, bf16[1,256,16,128]{3,1,2,0:T(8,128)(2,1)} %get-tuple-element.19, bf16[1,256,16,128]{3,1,2,0:T(8,128)(2,1)S(1)} %get-tuple-element.18, f32[128]{0:T(128)S(1)} %fusion.177), kind=kOutput, calls=%fused_computation.31 | convolution fusion | flops 1624768512 | bytes 22020608 | tf_op jit(solution)/shard_map/...zwk,kx->...zwx/dot_general | solution.py:54
  444.8 12.1 %convolution_subtract_fusion = f32[3,16,256,256]{3,2,1,0:T(8,128)} fusion(f32[3,16,256,256]{3,2,1,0:T(8,128)} %fusion.12, f32[256,3,16,128]{3,0,2,1:T(8,128)} %fusion.55, bf16[1,256,16,128]{3,1,2,0:T(8,128)(2,1)} %copy.71, bf16[1,256,16,128]{3,1,2,0:T(8,128)(2,1)} %get-tuple-element.19, bf16[1,256,16,128]{3,1,2,0:T(8,128)(2,1)S(1)} %get-tuple-element.18, ...), kind=kOutput, calls=%fused_computation.10 | convolution fusion | flops 1627914240 | bytes 34603520 | tf_op jit(solution)/shard_map/...zwk,kx->...zwx/dot_general | solution.py:54
  456.9 7.2 %fusion.42 = bf16[16,256,256]{2,1,0:T(8,128)(2,1)S(1)} fusion(f32[3,16,256,256]{3,2,1,0:T(8,128)} %convolution_subtract_fusion, bf16[3,16,256,256]{3,2,1,0:T(8,128)(2,1)} %all-gather.2.cloned.1.call-done), kind=kLoop, calls=%fused_computation.59 | loop fusion | flops 9437184 | bytes 20971520 | tf_op jit(solution)/shard_map/add | solution.py:125
  467.8 2.7 fusion.84
  471.9 1.6 copy.72
  473.5 6.4 %all-to-all-start.5 = ((bf16[256,16,128]{2,1,0:T(8,128)(2,1)}), bf16[256,16,128]{2,1,0:T(8,128)(2,1)}, u32[]{:S(2)}, u32[]{:S(2)}) async-start(bf16[256,16,128]{2,1,0:T(8,128)(2,1)} %copy.72), calls=%async_computation.5 | async-start | bytes 2097152 | tf_op jit(solution)/shard_map/all_to_all | solution.py:139
  480.0 2.9 subtract_convert_fusion.4
  486.0 19.3 %collective-permute-start.16 = (bf16[1,16,16,128]{3,1,0,2:T(8,128)(2,1)S(1)}, bf16[1,16,16,128]{3,1,0,2:T(8,128)(2,1)S(1)}, u32[]{:S(2)}, u32[]{:S(2)}) collective-permute-start(bf16[1,16,16,128]{3,1,0,2:T(8,128)(2,1)S(1)} %get-tuple-element.47), channel_id=1, source_target_pairs={{0,4},{2,6},{4,8},{6,10},{8,12},{10,14},{12,16},{14,18},{16,20},{1... | collective-permute-start | bytes 196616 | tf_op jit(solution)/shard_map/ppermute | solution.py:28
  505.3 2.2 collective-permute-start.17
  507.6 1.9 collective-permute-start.20
  509.5 3.2 collective-permute-start.21
  512.8 2.7 collective-permute-start.22
  516.5 2.4 collective-permute-start.24
  518.9 4.6 collective-permute-start.25
  523.5 3.6 collective-permute-start.26
  527.1 2.9 collective-permute-start.27
  531.5 1.8 collective-permute-done.28
  539.3 2.1 fusion.39
  541.5 2.1 fusion.35
  543.5 2.3 maximum_bitcast_fusion
  (166 shorter events, 64.8 us)
Async XLA Ops:
  7.2 3.5 copy-start
  11.2 1.6 copy-start.11
  17.1 52.7 %all-to-all-start.1 = ((bf16[2,16,256,128]{3,1,0,2:T(8,128)(2,1)}), bf16[2,16,256,128]{3,1,0,2:T(8,128)(2,1)}, u32[]{:S(2)}, u32[]{:S(2)}) async-start(bf16[2,16,256,128]{3,1,0,2:T(8,128)(2,1)} %copy.46), calls=%async_computation.1 | async-start | bytes 4194304 | tf_op jit(solution)/shard_map/all_to_all | solution.py:113
  23.7 1.6 copy-start.12
  69.9 52.3 %all-to-all-start = ((bf16[2,16,256,128]{3,1,0,2:T(8,128)(2,1)}), bf16[2,16,256,128]{3,1,0,2:T(8,128)(2,1)S(1)}, u32[]{:S(2)}, u32[]{:S(2)}) async-start(bf16[2,16,256,128]{3,1,0,2:T(8,128)(2,1)} %copy.41), calls=%async_computation | async-start | bytes 4194304 | tf_op jit(solution)/shard_map/all_to_all | solution.py:114
  76.0 83.2 %all-gather.2.cloned.1.call-start = ((), (), s32[]{:S(2)}) async-start(), calls=%async_computation.6 | async-start | bytes 9437184 | tf_op jit(solution)/shard_map/all_gather | solution.py:92
  123.5 1.6 copy-start.14
  125.3 1.2 copy-start.15
  177.0 118.3 %all-to-all-start.2 = ((bf16[256,16,128]{2,1,0:T(8,128)(2,1)}), bf16[256,16,128]{2,1,0:T(8,128)(2,1)}, u32[]{:S(2)}, u32[]{:S(2)}) async-start(bf16[256,16,128]{2,1,0:T(8,128)(2,1)} %copy.55), calls=%async_computation.2 | async-start | bytes 2097152 | tf_op jit(solution)/shard_map/all_to_all | solution.py:139
  183.5 4.7 copy-start.1
  186.7 39.9 %collective-permute-start = (bf16[1,16,16,128]{3,1,0,2:T(8,128)(2,1)S(1)}, bf16[1,16,16,128]{3,1,0,2:T(8,128)(2,1)S(1)}, u32[]{:S(2)}, u32[]{:S(2)}) collective-permute-start(bf16[1,16,16,128]{3,1,0,2:T(8,128)(2,1)S(1)} %constant_dynamic-slice_fusion.29), channel_id=1, source_target_pairs={{0,2},{2,4},{4,6},{6,8},{8,10},{10,12},{12,14},{14,16},{16,18},{18... | collective-permute-start | bytes 196616 | tf_op jit(solution)/shard_map/ppermute | solution.py:28
  189.8 40.0 %copy-start.16 = (f32[64]{0:T(128)S(1)}, f32[64]{0:T(128)}, u32[]{:S(2)}) copy-start(f32[64]{0:T(128)} %param.8) | copy-start | bytes 772
  226.9 44.8 %collective-permute-start.1 = (bf16[1,16,16,128]{3,1,0,2:T(8,128)(2,1)S(1)}, bf16[1,16,16,128]{3,1,0,2:T(8,128)(2,1)S(1)}, u32[]{:S(2)}, u32[]{:S(2)}) collective-permute-start(bf16[1,16,16,128]{3,1,0,2:T(8,128)(2,1)S(1)} %get-tuple-element.62), channel_id=1, source_target_pairs={{0,4},{2,6},{4,8},{6,10},{8,12},{10,14},{12,16},{14,18},{16,20},{1... | collective-permute-start | bytes 196616 | tf_op jit(solution)/shard_map/ppermute | solution.py:28
  256.8 15.3 %collective-permute-start.2 = (bf16[1,16,16,128]{3,1,0,2:T(8,128)(2,1)S(1)}, bf16[1,16,16,128]{3,1,0,2:T(8,128)(2,1)S(1)}, u32[]{:S(2)}, u32[]{:S(2)}) collective-permute-start(bf16[1,16,16,128]{3,1,0,2:T(8,128)(2,1)S(1)} %get-tuple-element.61), channel_id=1, source_target_pairs={{0,6},{2,8},{4,10},{6,12},{8,14},{10,16},{12,18},{14,20},{16,22},{... | collective-permute-start | bytes 196616 | tf_op jit(solution)/shard_map/ppermute | solution.py:28
  258.8 15.9 %collective-permute-start.3 = (bf16[1,16,16,128]{3,1,0,2:T(8,128)(2,1)S(1)}, bf16[1,16,16,128]{3,1,0,2:T(8,128)(2,1)S(1)}, u32[]{:S(2)}, u32[]{:S(2)}) collective-permute-start(bf16[1,16,16,128]{3,1,0,2:T(8,128)(2,1)S(1)} %get-tuple-element.60), channel_id=1, source_target_pairs={{0,8},{2,10},{4,12},{6,14},{8,16},{10,18},{12,20},{14,22},{16,24},... | collective-permute-start | bytes 196616 | tf_op jit(solution)/shard_map/ppermute | solution.py:28
  261.9 14.9 %collective-permute-start.4 = (bf16[1,16,16,128]{3,1,0,2:T(8,128)(2,1)S(1)}, bf16[1,16,16,128]{3,1,0,2:T(8,128)(2,1)S(1)}, u32[]{:S(2)}, u32[]{:S(2)}) collective-permute-start(bf16[1,16,16,128]{3,1,0,2:T(8,128)(2,1)S(1)} %get-tuple-element.59), channel_id=1, source_target_pairs={{0,10},{2,12},{4,14},{6,16},{8,18},{10,20},{12,22},{14,24},{16,26}... | collective-permute-start | bytes 196616 | tf_op jit(solution)/shard_map/ppermute | solution.py:28
  268.8 10.0 %collective-permute-start.5 = (bf16[1,16,16,128]{3,1,0,2:T(8,128)(2,1)S(1)}, bf16[1,16,16,128]{3,1,0,2:T(8,128)(2,1)S(1)}, u32[]{:S(2)}, u32[]{:S(2)}) collective-permute-start(bf16[1,16,16,128]{3,1,0,2:T(8,128)(2,1)S(1)} %get-tuple-element.58), channel_id=1, source_target_pairs={{0,12},{2,14},{4,16},{6,18},{8,20},{10,22},{12,24},{14,26},{16,28}... | collective-permute-start | bytes 196616 | tf_op jit(solution)/shard_map/ppermute | solution.py:28
  271.7 8.4 %collective-permute-start.6 = (bf16[1,16,16,128]{3,1,0,2:T(8,128)(2,1)S(1)}, bf16[1,16,16,128]{3,1,0,2:T(8,128)(2,1)S(1)}, u32[]{:S(2)}, u32[]{:S(2)}) collective-permute-start(bf16[1,16,16,128]{3,1,0,2:T(8,128)(2,1)S(1)} %get-tuple-element.57), channel_id=1, source_target_pairs={{0,14},{2,16},{4,18},{6,20},{8,22},{10,24},{12,26},{14,28},{16,30}... | collective-permute-start | bytes 196616 | tf_op jit(solution)/shard_map/ppermute | solution.py:28
  272.0 11.5 %collective-permute-start.7 = (bf16[1,16,16,128]{3,1,0,2:T(8,128)(2,1)S(1)}, bf16[1,16,16,128]{3,1,0,2:T(8,128)(2,1)S(1)}, u32[]{:S(2)}, u32[]{:S(2)}) collective-permute-start(bf16[1,16,16,128]{3,1,0,2:T(8,128)(2,1)S(1)} %get-tuple-element.56), channel_id=1, source_target_pairs={{0,16},{2,18},{4,20},{6,22},{8,24},{10,26},{12,28},{14,30},{16,0},... | collective-permute-start | bytes 196616 | tf_op jit(solution)/shard_map/ppermute | solution.py:28
  274.6 15.7 %collective-permute-start.8 = (bf16[1,16,16,128]{3,1,0,2:T(8,128)(2,1)S(1)}, bf16[1,16,16,128]{3,1,0,2:T(8,128)(2,1)S(1)}, u32[]{:S(2)}, u32[]{:S(2)}) collective-permute-start(bf16[1,16,16,128]{3,1,0,2:T(8,128)(2,1)S(1)} %get-tuple-element.55), channel_id=1, source_target_pairs={{0,18},{2,20},{4,22},{6,24},{8,26},{10,28},{12,30},{14,0},{16,2},{... | collective-permute-start | bytes 196616 | tf_op jit(solution)/shard_map/ppermute | solution.py:28
  276.8 13.6 %collective-permute-start.9 = (bf16[1,16,16,128]{3,1,0,2:T(8,128)(2,1)S(1)}, bf16[1,16,16,128]{3,1,0,2:T(8,128)(2,1)S(1)}, u32[]{:S(2)}, u32[]{:S(2)}) collective-permute-start(bf16[1,16,16,128]{3,1,0,2:T(8,128)(2,1)S(1)} %get-tuple-element.54), channel_id=1, source_target_pairs={{0,20},{2,22},{4,24},{6,26},{8,28},{10,30},{12,0},{14,2},{16,4},{1... | collective-permute-start | bytes 196616 | tf_op jit(solution)/shard_map/ppermute | solution.py:28
  278.8 13.5 %collective-permute-start.10 = (bf16[1,16,16,128]{3,1,0,2:T(8,128)(2,1)S(1)}, bf16[1,16,16,128]{3,1,0,2:T(8,128)(2,1)S(1)}, u32[]{:S(2)}, u32[]{:S(2)}) collective-permute-start(bf16[1,16,16,128]{3,1,0,2:T(8,128)(2,1)S(1)} %get-tuple-element.53), channel_id=1, source_target_pairs={{0,22},{2,24},{4,26},{6,28},{8,30},{10,0},{12,2},{14,4},{16,6},{18... | collective-permute-start | bytes 196616 | tf_op jit(solution)/shard_map/ppermute | solution.py:28
  280.2 12.2 %collective-permute-start.11 = (bf16[1,16,16,128]{3,1,0,2:T(8,128)(2,1)S(1)}, bf16[1,16,16,128]{3,1,0,2:T(8,128)(2,1)S(1)}, u32[]{:S(2)}, u32[]{:S(2)}) collective-permute-start(bf16[1,16,16,128]{3,1,0,2:T(8,128)(2,1)S(1)} %get-tuple-element.52), channel_id=1, source_target_pairs={{0,24},{2,26},{4,28},{6,30},{8,0},{10,2},{12,4},{14,6},{16,8},{18,... | collective-permute-start | bytes 196616 | tf_op jit(solution)/shard_map/ppermute | solution.py:28
  283.5 8.9 %collective-permute-start.12 = (bf16[1,16,16,128]{3,1,0,2:T(8,128)(2,1)S(1)}, bf16[1,16,16,128]{3,1,0,2:T(8,128)(2,1)S(1)}, u32[]{:S(2)}, u32[]{:S(2)}) collective-permute-start(bf16[1,16,16,128]{3,1,0,2:T(8,128)(2,1)S(1)} %get-tuple-element.51), channel_id=1, source_target_pairs={{0,26},{2,28},{4,30},{6,0},{8,2},{10,4},{12,6},{14,8},{16,10},{18,... | collective-permute-start | bytes 196616 | tf_op jit(solution)/shard_map/ppermute | solution.py:28
  290.4 3.7 collective-permute-start.13
  290.5 4.2 collective-permute-start.14
  301.0 1.5 copy-start.4
  301.1 2.9 copy-start.2
  305.4 1.6 copy-start.6
  305.4 1.6 copy-start.7
  305.4 1.6 copy-start.9
  311.6 52.1 %all-to-all-start.4 = ((bf16[2,16,256,128]{3,1,0,2:T(8,128)(2,1)}), bf16[2,16,256,128]{3,1,0,2:T(8,128)(2,1)}, u32[]{:S(2)}, u32[]{:S(2)}) async-start(bf16[2,16,256,128]{3,1,0,2:T(8,128)(2,1)} %copy.63), calls=%async_computation.4 | async-start | bytes 4194304 | tf_op jit(solution)/shard_map/all_to_all | solution.py:113
  317.5 3.0 copy-start.8
  317.5 3.0 copy-start.10
  363.7 52.3 %all-to-all-start.3 = ((bf16[2,16,256,128]{3,1,0,2:T(8,128)(2,1)}), bf16[2,16,256,128]{3,1,0,2:T(8,128)(2,1)}, u32[]{:S(2)}, u32[]{:S(2)}) async-start(bf16[2,16,256,128]{3,1,0,2:T(8,128)(2,1)} %copy.58), calls=%async_computation.3 | async-start | bytes 4194304 | tf_op jit(solution)/shard_map/all_to_all | solution.py:114
  429.0 1.8 copy-start.13
  473.5 61.1 %all-to-all-start.5 = ((bf16[256,16,128]{2,1,0:T(8,128)(2,1)}), bf16[256,16,128]{2,1,0:T(8,128)(2,1)}, u32[]{:S(2)}, u32[]{:S(2)}) async-start(bf16[256,16,128]{2,1,0:T(8,128)(2,1)} %copy.72), calls=%async_computation.5 | async-start | bytes 2097152 | tf_op jit(solution)/shard_map/all_to_all | solution.py:139
  482.9 2.8 collective-permute-start.15
  486.0 23.5 %collective-permute-start.16 = (bf16[1,16,16,128]{3,1,0,2:T(8,128)(2,1)S(1)}, bf16[1,16,16,128]{3,1,0,2:T(8,128)(2,1)S(1)}, u32[]{:S(2)}, u32[]{:S(2)}) collective-permute-start(bf16[1,16,16,128]{3,1,0,2:T(8,128)(2,1)S(1)} %get-tuple-element.47), channel_id=1, source_target_pairs={{0,4},{2,6},{4,8},{6,10},{8,12},{10,14},{12,16},{14,18},{16,20},{1... | collective-permute-start | bytes 196616 | tf_op jit(solution)/shard_map/ppermute | solution.py:28
  505.3 7.4 %collective-permute-start.17 = (bf16[1,16,16,128]{3,1,0,2:T(8,128)(2,1)S(1)}, bf16[1,16,16,128]{3,1,0,2:T(8,128)(2,1)S(1)}, u32[]{:S(2)}, u32[]{:S(2)}) collective-permute-start(bf16[1,16,16,128]{3,1,0,2:T(8,128)(2,1)S(1)} %get-tuple-element.46), channel_id=1, source_target_pairs={{0,6},{2,8},{4,10},{6,12},{8,14},{10,16},{12,18},{14,20},{16,22},{... | collective-permute-start | bytes 196616 | tf_op jit(solution)/shard_map/ppermute | solution.py:28
  507.5 8.0 %collective-permute-start.18 = (bf16[1,16,16,128]{3,1,0,2:T(8,128)(2,1)S(1)}, bf16[1,16,16,128]{3,1,0,2:T(8,128)(2,1)S(1)}, u32[]{:S(2)}, u32[]{:S(2)}) collective-permute-start(bf16[1,16,16,128]{3,1,0,2:T(8,128)(2,1)S(1)} %get-tuple-element.45), channel_id=1, source_target_pairs={{0,8},{2,10},{4,12},{6,14},{8,16},{10,18},{12,20},{14,22},{16,24},... | collective-permute-start | bytes 196616 | tf_op jit(solution)/shard_map/ppermute | solution.py:28
  507.5 9.0 %collective-permute-start.19 = (bf16[1,16,16,128]{3,1,0,2:T(8,128)(2,1)S(1)}, bf16[1,16,16,128]{3,1,0,2:T(8,128)(2,1)S(1)}, u32[]{:S(2)}, u32[]{:S(2)}) collective-permute-start(bf16[1,16,16,128]{3,1,0,2:T(8,128)(2,1)S(1)} %get-tuple-element.44), channel_id=1, source_target_pairs={{0,10},{2,12},{4,14},{6,16},{8,18},{10,20},{12,22},{14,24},{16,26}... | collective-permute-start | bytes 196616 | tf_op jit(solution)/shard_map/ppermute | solution.py:28
  507.6 11.3 %collective-permute-start.20 = (bf16[1,16,16,128]{3,1,0,2:T(8,128)(2,1)S(1)}, bf16[1,16,16,128]{3,1,0,2:T(8,128)(2,1)S(1)}, u32[]{:S(2)}, u32[]{:S(2)}) collective-permute-start(bf16[1,16,16,128]{3,1,0,2:T(8,128)(2,1)S(1)} %get-tuple-element.43), channel_id=1, source_target_pairs={{0,12},{2,14},{4,16},{6,18},{8,20},{10,22},{12,24},{14,26},{16,28}... | collective-permute-start | bytes 196616 | tf_op jit(solution)/shard_map/ppermute | solution.py:28
  509.5 14.0 %collective-permute-start.21 = (bf16[1,16,16,128]{3,1,0,2:T(8,128)(2,1)S(1)}, bf16[1,16,16,128]{3,1,0,2:T(8,128)(2,1)S(1)}, u32[]{:S(2)}, u32[]{:S(2)}) collective-permute-start(bf16[1,16,16,128]{3,1,0,2:T(8,128)(2,1)S(1)} %get-tuple-element.42), channel_id=1, source_target_pairs={{0,14},{2,16},{4,18},{6,20},{8,22},{10,24},{12,26},{14,28},{16,30}... | collective-permute-start | bytes 196616 | tf_op jit(solution)/shard_map/ppermute | solution.py:28
  512.8 14.4 %collective-permute-start.22 = (bf16[1,16,16,128]{3,1,0,2:T(8,128)(2,1)S(1)}, bf16[1,16,16,128]{3,1,0,2:T(8,128)(2,1)S(1)}, u32[]{:S(2)}, u32[]{:S(2)}) collective-permute-start(bf16[1,16,16,128]{3,1,0,2:T(8,128)(2,1)S(1)} %get-tuple-element.41), channel_id=1, source_target_pairs={{0,16},{2,18},{4,20},{6,22},{8,24},{10,26},{12,28},{14,30},{16,0},... | collective-permute-start | bytes 196616 | tf_op jit(solution)/shard_map/ppermute | solution.py:28
  515.5 14.6 %collective-permute-start.23 = (bf16[1,16,16,128]{3,1,0,2:T(8,128)(2,1)S(1)}, bf16[1,16,16,128]{3,1,0,2:T(8,128)(2,1)S(1)}, u32[]{:S(2)}, u32[]{:S(2)}) collective-permute-start(bf16[1,16,16,128]{3,1,0,2:T(8,128)(2,1)S(1)} %get-tuple-element.40), channel_id=1, source_target_pairs={{0,18},{2,20},{4,22},{6,24},{8,26},{10,28},{12,30},{14,0},{16,2},{... | collective-permute-start | bytes 196616 | tf_op jit(solution)/shard_map/ppermute | solution.py:28
  516.5 13.7 %collective-permute-start.24 = (bf16[1,16,16,128]{3,1,0,2:T(8,128)(2,1)S(1)}, bf16[1,16,16,128]{3,1,0,2:T(8,128)(2,1)S(1)}, u32[]{:S(2)}, u32[]{:S(2)}) collective-permute-start(bf16[1,16,16,128]{3,1,0,2:T(8,128)(2,1)S(1)} %get-tuple-element.39), channel_id=1, source_target_pairs={{0,20},{2,22},{4,24},{6,26},{8,28},{10,30},{12,0},{14,2},{16,4},{1... | collective-permute-start | bytes 196616 | tf_op jit(solution)/shard_map/ppermute | solution.py:28
  518.9 12.5 %collective-permute-start.25 = (bf16[1,16,16,128]{3,1,0,2:T(8,128)(2,1)S(1)}, bf16[1,16,16,128]{3,1,0,2:T(8,128)(2,1)S(1)}, u32[]{:S(2)}, u32[]{:S(2)}) collective-permute-start(bf16[1,16,16,128]{3,1,0,2:T(8,128)(2,1)S(1)} %get-tuple-element.38), channel_id=1, source_target_pairs={{0,22},{2,24},{4,26},{6,28},{8,30},{10,0},{12,2},{14,4},{16,6},{18... | collective-permute-start | bytes 196616 | tf_op jit(solution)/shard_map/ppermute | solution.py:28
  523.5 7.9 %collective-permute-start.26 = (bf16[1,16,16,128]{3,1,0,2:T(8,128)(2,1)S(1)}, bf16[1,16,16,128]{3,1,0,2:T(8,128)(2,1)S(1)}, u32[]{:S(2)}, u32[]{:S(2)}) collective-permute-start(bf16[1,16,16,128]{3,1,0,2:T(8,128)(2,1)S(1)} %get-tuple-element.37), channel_id=1, source_target_pairs={{0,24},{2,26},{4,28},{6,30},{8,0},{10,2},{12,4},{14,6},{16,8},{18,... | collective-permute-start | bytes 196616 | tf_op jit(solution)/shard_map/ppermute | solution.py:28
  527.1 4.3 collective-permute-start.27
  530.1 3.2 collective-permute-start.28
  530.2 3.8 collective-permute-start.29
  536.2 2.7 copy-start.3
  537.5 1.8 copy-start.5
Sparse Core Ops, SparseCore 0:
  78.3 80.8 all-gather.1
